TPU v7x, 256 devices: a whole 4x4x8 slice. The times are simulated.
256 devices in a mesh: gz: 64 (over z_hi, x, y), gx: 4 (over z_lo, core).
Axes of the slice: x: 4, y: 4, z: 8 (z_hi: 4, z_lo: 2; z = z_hi * 2 + z_lo), core: 2. Of those that a mesh axis runs over, the one named last changes fastest.
Arguments:
- density: float32 [512, 128, 128], P('gz', 'gx'), may hold values from -6 to 6
- velocity: float32 [3, 512, 128, 128], P(None, 'gz', 'gx'), may hold values from -6 to 6
- labels: int32 [512, 128, 128], P('gz', 'gx'), may hold values from 0 to 7
- sound_table: float32 [8], replicated, may hold values from 0.8 to 1.6
- mass_table: float32 [8], replicated, may hold values from 0.8 to 2
- source_index: int32 [4096], replicated, may hold values from 0 to 8388607
- source_values: float32 [1, 4096], replicated, may hold values from -6 to 6
Outputs:
- new_density: float32 [512, 128, 128], P('gz', 'gx')
- new_velocity: float32 [3, 512, 128, 128], P(None, 'gz', 'gx')
Inputs may be any that keep to these rules, and one draw needn't show every extreme that they name: `source_index`: flat cell index z * 128 * 128 + x * 128 + y; an index may repeat.
All inputs are finite; a program needn't handle non-finite values.
Results may differ from a plain program's by a relative error of at most 0.00011.
Values sent between devices are 32-bit elements; how exact they have to be, the bound alone decides.
A program may use at most 64 MiB of HBM per device.

v0:
```python
import math

import jax
import jax.numpy as jnp
import numpy as np
from jax import lax
from jax.experimental import pallas as pl
from jax.experimental.pallas import tpu as pltpu
from jax.sharding import PartitionSpec as P

NZ = 512
NX = 128
NY = 128
LABELS = 8
PML_W = 20
SRC = 4096
DT = 0.3
ABSORB = 2.0
G = 16
Z_LOC = 8
X_LOC = 32
ROWS = Z_LOC * X_LOC
MESH = pl.DeviceIdType.MESH
F32 = jnp.float32
BF16 = jnp.bfloat16

P_A, P_B, W0_B, WZ_B, U0_A, UX_A, UZ_A, VY_A, VX_A, VZ_A, QXY_B, QZ_B, S_B, S_A = range(14)


def basis(n):
    j = np.arange(n)
    f = np.concatenate([np.arange(n // 2 + 1), np.arange(1, n // 2)])
    is_sin = (np.arange(n) > n // 2)[:, None]
    scale = np.where((f == 0) | (f == n // 2), math.sqrt(1.0 / n), math.sqrt(2.0 / n))[:, None]
    k = (2.0 * math.pi / n * f)[:, None]
    phase = 2.0 * math.pi / n * ((f[:, None] * j[None, :]) % n)
    half = 2.0 * math.pi / (2 * n) * ((f[:, None] * (2 * j[None, :] + 1)) % (2 * n))
    forward = np.where(is_sin, np.sin(phase), np.cos(phase)) * scale
    slope = np.where(is_sin, k * np.cos(half), -k * np.sin(half)) * scale
    return forward, slope


def parts(table):
    table = table.astype(np.float32)
    high = table.astype(jnp.bfloat16)
    low = (table - high.astype(np.float32)).astype(jnp.bfloat16)
    return [high, low]


def tables():
    r, d = basis(NX)
    small = np.stack(parts(r) + parts(d))
    r, d = basis(NZ)
    lane = np.arange(NZ)
    z = (lane % 4) * 128 + (lane // 32) * Z_LOC + (lane % 32) // 4
    large = np.stack(parts(r[:, z]) + parts(d[:, z]))
    return small, large


def split(x):
    high = x.astype(BF16)
    return high, (x - high.astype(F32)).astype(BF16)


def product(a, b, dims):
    contract = (((1,), (0 if dims == "nn" else 1,)), ((), ()))

    def dot(u, v):
        return lax.dot_general(u, v, contract, preferred_element_type=F32)

    return dot(a[0], b[0]) + dot(a[1], b[0]) + dot(a[0], b[1])


def swap_blocks(a):
    lane = lax.broadcasted_iota(jnp.int32, a[0].shape, 1)
    low_half = lane < 64
    even = (lane % 64) < 32

    def far(u, v):
        return (
            jnp.where(low_half, u, pltpu.roll(v, 64, 1)),
            jnp.where(low_half, pltpu.roll(u, 64, 1), v),
        )

    def near(u, v):
        return (
            jnp.where(even, u, pltpu.roll(v, 32, 1)),
            jnp.where(even, pltpu.roll(u, 96, 1), v),
        )

    c0, c2 = far(a[0], a[2])
    c1, c3 = far(a[1], a[3])
    b0, b1 = near(c0, c1)
    b2, b3 = near(c2, c3)
    return b0, b1, b2, b3


def kernel(
    sound, mass, dens_hbm, vel_hbm, lab_hbm, sidx, sval, small, large_hbm,
    out_d, out_v,
    send_buf, recv_buf, work, long_a, long_b, dens, vel, lab, large,
    base_v, coef_v, base_d, coef_d, corr, row_of, col_of,
    send_sem, recv_sem, load_sem, out_sem,
):
    gz = lax.axis_index("gz")
    gx = lax.axis_index("gx")
    z_hi = lax.div(gz, 16)
    me_b = lax.rem(gz, 16)
    me_a = z_hi * 4 + gx

    def device_of(group, peer):
        if group == "A":
            return (lax.div(peer, 4) * 16 + me_b, lax.rem(peer, 4))
        return (z_hi * 16 + peer, gx)

    loads = [
        pltpu.make_async_copy(lab_hbm, lab, load_sem.at[0]),
        pltpu.make_async_copy(dens_hbm, dens, load_sem.at[1]),
        pltpu.make_async_copy(vel_hbm, vel, load_sem.at[2]),
        pltpu.make_async_copy(large_hbm, large, load_sem.at[3]),
    ]
    for load in loads:
        load.start()

    barrier = pltpu.get_barrier_semaphore()

    def greet(step, carry):
        for group, me in (("A", me_a), ("B", me_b)):
            peer = lax.rem(me + step, G)
            pl.semaphore_signal(
                barrier, inc=1, device_id=device_of(group, peer), device_id_type=MESH
            )
        return carry

    lax.fori_loop(1, G, greet, 0)

    def send(which, group):
        me = me_a if group == "A" else me_b
        recv_buf[which, me] = send_buf[which, me]

        def one(step, carry):
            peer = lax.rem(me + step, G)
            pltpu.make_async_remote_copy(
                send_buf.at[which, peer],
                recv_buf.at[which, me],
                send_sem.at[which],
                recv_sem.at[which],
                device_id=device_of(group, peer),
                device_id_type=MESH,
            ).start()
            return carry

        lax.fori_loop(1, G, one, 0)

    def whole(which):
        return pltpu.make_async_copy(
            send_buf.at[which, pl.ds(0, G - 1)],
            recv_buf.at[which, pl.ds(0, G - 1)],
            recv_sem.at[which],
        )

    def arrived(which):
        whole(which).wait()

    def sent(which):
        pltpu.make_async_copy(
            send_buf.at[which, pl.ds(0, G - 1)],
            recv_buf.at[which, pl.ds(0, G - 1)],
            send_sem.at[which],
        ).wait()

    r_small = (small[0], small[1])
    d_small = (small[2], small[3])

    def put(which, value):
        send_buf[which] = value.reshape(G, 8, ROWS)

    def to_x_lines(which):
        got = recv_buf[which].reshape(4, 4, 8, ROWS)
        for tile in range(2):
            a = [got[:, g, :, tile * 128 : tile * 128 + 128].reshape(32, 128) for g in range(4)]
            for q, b in enumerate(swap_blocks(a)):
                work[pl.ds((tile * 4 + q) * 32, 32), :] = b
        return jnp.concatenate([work[pl.ds(ky, 32, stride=8), :] for ky in range(8)], axis=0)

    def from_x_lines(which, value):
        for ky in range(8):
            work[pl.ds(ky, 32, stride=8), :] = value[ky * 32 : ky * 32 + 32]
        for tile in range(2):
            b = [work[pl.ds((tile * 4 + q) * 32, 32), :] for q in range(4)]
            for g, a in enumerate(swap_blocks(b)):
                a = a.reshape(4, 8, 128)
                for high in range(4):
                    send_buf[which, high * 4 + g, :, tile * 128 : tile * 128 + 128] = a[high]

    def to_z_lines(which, place):
        got = recv_buf[which].reshape(4, 4, 8, ROWS)
        for tile in range(2):
            a = [got[:, g, :, tile * 128 : tile * 128 + 128].reshape(32, 128) for g in range(4)]
            for q, b in enumerate(swap_blocks(a)):
                b = b.reshape(4, 8, 128)
                for high in range(4):
                    place[(tile * 4 + q) * 8 : (tile * 4 + q) * 8 + 8, high * 128 : high * 128 + 128] = b[high]
        return place[...]

    def from_z_lines(which, value):
        for tile in range(2):
            b = []
            for q in range(4):
                rows = value[(tile * 4 + q) * 8 : (tile * 4 + q) * 8 + 8]
                b.append(jnp.concatenate([rows[:, h * 128 : h * 128 + 128] for h in range(4)], axis=0))
            for g, a in enumerate(swap_blocks(b)):
                a = a.reshape(4, 8, 128)
                for high in range(4):
                    send_buf[which, high * 4 + g, :, tile * 128 : tile * 128 + 128] = a[high]

    def turned(which):
        return split(recv_buf[which].reshape(G * 8, ROWS).T)

    speed_ref = sound[0]
    for tissue in range(1, LABELS):
        speed_ref = jnp.maximum(speed_ref, sound[tissue])

    loads[0].wait()
    loads[1].wait()
    classes = lab[...].reshape(ROWS, NY)
    speed = jnp.full((ROWS, NY), sound[0])
    for tissue in range(1, LABELS):
        speed = jnp.where(classes == tissue, sound[tissue], speed)
    pressure = speed * speed * dens[...].reshape(ROWS, NY)
    put(P_A, product(r_small, split(pressure), "nt"))
    pl.semaphore_wait(barrier, 2 * (G - 1))
    send(P_A, "A")

    loads[2].wait()
    density_mass = jnp.full((ROWS, NY), mass[0])
    for tissue in range(1, LABELS):
        density_mass = jnp.where(classes == tissue, mass[tissue], density_mass)
    row = lax.broadcasted_iota(jnp.int32, (ROWS, NY), 0)
    col = lax.broadcasted_iota(jnp.int32, (ROWS, NY), 1)

    def damping(position, length):
        coordinate = position.astype(F32)
        depth = jnp.maximum(
            jnp.maximum(PML_W - coordinate, coordinate - (length - 1 - PML_W)), 0.0
        ) / PML_W
        square = depth * depth
        return jnp.exp(-ABSORB * speed_ref * (square * square) * DT * 0.5)

    damp = (
        damping(gz * Z_LOC + row // X_LOC, NZ),
        damping(gx * X_LOC + row % X_LOC, NX),
        damping(col, NY),
    )
    over_mass = DT / density_mass
    for a in range(3):
        base_v[a] = damp[a] * (damp[a] * vel[a].reshape(ROWS, NY))
        coef_v[a] = damp[a] * over_mass
    damp_all = damp[0] * damp[1] * damp[2]
    base_d[...] = damp_all * (damp_all * dens[...].reshape(ROWS, NY))
    coef_d[...] = damp_all * (DT * density_mass)

    line = lax.broadcasted_iota(jnp.int32, (64, NZ), 0)
    index_z = lax.broadcasted_iota(jnp.int32, (64, NZ), 1)

    def wave(index, length):
        folded = jnp.where(index <= length // 2, index, index - length // 2)
        return folded.astype(F32) * (2.0 * math.pi / length)

    wz = wave(index_z, NZ)
    wx = wave(me_b * 8 + line % 8, NX)
    wy = wave(me_a * 8 + line // 8, NY)
    angle = speed_ref * jnp.sqrt(wz * wz + wx * wx + wy * wy) * (DT / 2.0)
    at_zero = angle == 0.0
    safe = jnp.where(at_zero, 1.0, angle)
    corr[...] = jnp.where(at_zero, 1.0, jnp.sin(safe) / safe)

    arrived(P_A)
    put(P_B, product(r_small, split(to_x_lines(P_A)), "nt"))
    send(P_B, "B")

    where = sidx[...]
    plane = NX * NY
    z_off = where // plane - gz * Z_LOC
    remain = where % plane
    x_off = remain // NY - gx * X_LOC
    inside = (z_off >= 0) & (z_off < Z_LOC) & (x_off >= 0) & (x_off < X_LOC)
    row_of[...] = jnp.where(inside, z_off * X_LOC + x_off, -1)
    col_of[...] = remain % NY

    def add_some(step, carry):
        picks = []
        highs = []
        lows = []
        for part in range(2):
            at = pl.ds(step * 2 + part, 1)
            picks.append(jnp.where(row == row_of[at, :], 1.0, 0.0).astype(BF16))
            amount = jnp.where(row[:NY] == col_of[at, :], sval[at, :], 0.0)
            high, low = split(amount)
            highs.append(high)
            lows.append(low)
        pick = jnp.concatenate(picks, axis=1)
        contract = (((1,), (1,)), ((), ()))
        high = lax.dot_general(pick, jnp.concatenate(highs, axis=1), contract, preferred_element_type=F32)
        low = lax.dot_general(pick, jnp.concatenate(lows, axis=1), contract, preferred_element_type=F32)
        base_d[...] += high + low
        return carry

    lax.fori_loop(0, SRC // NY // 2, add_some, 0)

    loads[3].wait()
    r_large = (large[0], large[1])
    d_large = (large[2], large[3])

    arrived(P_B)
    spectrum = product(split(to_z_lines(P_B, long_a)), r_large, "nt")
    spectrum = split(spectrum * corr[...])
    from_z_lines(W0_B, product(spectrum, r_large, "nn"))
    send(W0_B, "B")
    from_z_lines(WZ_B, product(spectrum, d_large, "nn"))
    send(WZ_B, "B")

    arrived(W0_B)
    field = turned(W0_B)
    from_x_lines(U0_A, product(field, r_small, "nn"))
    send(U0_A, "A")
    from_x_lines(UX_A, product(field, d_small, "nn"))
    send(UX_A, "A")
    arrived(WZ_B)
    from_x_lines(UZ_A, product(turned(WZ_B), r_small, "nn"))
    send(UZ_A, "A")

    stores = []
    for came, goes, a, back, sign in (
        (U0_A, VY_A, 2, d_small, -1),
        (UX_A, VX_A, 1, r_small, 1),
        (UZ_A, VZ_A, 0, r_small, 1),
    ):
        arrived(came)
        slope = product(turned(came), back, "nn")
        fresh = base_v[a] - coef_v[a] * slope
        halves = split(fresh)
        if sign > 0:
            put(goes, product(r_small, halves, "nt"))
        else:
            put(goes, -product(d_small, halves, "nt"))
        send(goes, "A")
        vel[a] = fresh.reshape(Z_LOC, X_LOC, NY)
        store = pltpu.make_async_copy(vel.at[a], out_v.at[a], out_sem.at[a])
        store.start()
        stores.append(store)

    arrived(VY_A)
    part_y = product(r_small, split(to_x_lines(VY_A)), "nt")
    arrived(VX_A)
    put(QXY_B, part_y - product(d_small, split(to_x_lines(VX_A)), "nt"))
    send(QXY_B, "B")
    arrived(VZ_A)
    put(QZ_B, product(r_small, split(to_x_lines(VZ_A)), "nt"))
    send(QZ_B, "B")

    arrived(QXY_B)
    spectrum = product(split(to_z_lines(QXY_B, long_a)), r_large, "nt")
    arrived(QZ_B)
    spectrum = spectrum - product(split(to_z_lines(QZ_B, long_b)), d_large, "nt")
    from_z_lines(S_B, product(split(spectrum * corr[...]), r_large, "nn"))
    send(S_B, "B")

    arrived(S_B)
    from_x_lines(S_A, product(turned(S_B), r_small, "nn"))
    send(S_A, "A")

    arrived(S_A)
    spread = product(turned(S_A), r_small, "nn")
    dens[...] = (base_d[...] - coef_d[...] * spread).reshape(Z_LOC, X_LOC, NY)
    store = pltpu.make_async_copy(dens, out_d, out_sem.at[3])
    store.start()
    stores.append(store)
    for which in range(14):
        sent(which)
    for store in stores:
        store.wait()


def shards(density, velocity, labels, sound_table, mass_table, source_index, source_values):
    small, large = tables()
    block = (G, 8, ROWS)
    vmem = pl.BlockSpec(memory_space=pltpu.VMEM)
    smem = pl.BlockSpec(memory_space=pltpu.SMEM)
    anyspace = pl.BlockSpec(memory_space=pl.ANY)
    field = (Z_LOC, X_LOC, NY)
    return pl.pallas_call(
        kernel,
        out_shape=(
            jax.ShapeDtypeStruct(field, F32),
            jax.ShapeDtypeStruct((3,) + field, F32),
        ),
        in_specs=[smem, smem, anyspace, anyspace, anyspace, vmem, vmem, vmem, anyspace],
        out_specs=(anyspace, anyspace),
        scratch_shapes=[
            pltpu.VMEM((14,) + block, F32),
            pltpu.VMEM((14,) + block, F32),
            pltpu.VMEM((ROWS, NY), F32),
            pltpu.VMEM((64, NZ), F32),
            pltpu.VMEM((64, NZ), F32),
            pltpu.VMEM(field, F32),
            pltpu.VMEM((3,) + field, F32),
            pltpu.VMEM(field, jnp.int32),
            pltpu.VMEM((4, NZ, NZ), BF16),
            pltpu.VMEM((3, ROWS, NY), F32),
            pltpu.VMEM((3, ROWS, NY), F32),
            pltpu.VMEM((ROWS, NY), F32),
            pltpu.VMEM((ROWS, NY), F32),
            pltpu.VMEM((64, NZ), F32),
            pltpu.VMEM((SRC // NY, NY), jnp.int32),
            pltpu.VMEM((SRC // NY, NY), jnp.int32),
            pltpu.SemaphoreType.DMA((14,)),
            pltpu.SemaphoreType.DMA((14,)),
            pltpu.SemaphoreType.DMA((4,)),
            pltpu.SemaphoreType.DMA((4,)),
        ],
        compiler_params=pltpu.CompilerParams(collective_id=0, has_side_effects=True),
    )(
        sound_table,
        mass_table,
        density,
        velocity,
        labels,
        source_index.reshape(SRC // NY, NY),
        source_values[0].reshape(SRC // NY, NY),
        jnp.asarray(small),
        jnp.asarray(large),
    )


def solution(mesh):
    in_specs = (
        P("gz", "gx", None),
        P(None, "gz", "gx", None),
        P("gz", "gx", None),
        P(),
        P(),
        P(),
        P(),
    )
    out_specs = (P("gz", "gx", None), P(None, "gz", "gx", None))
    return jax.shard_map(shards, mesh=mesh, in_specs=in_specs, out_specs=out_specs, check_vma=False)
```

profile of v0, /device:TPU:1, one launch (start us, length us, event | category | flops | bytes accessed | tf_op | source)
XLA Modules:
  0.0 73.8 jit_solution(3038551377414985782)
XLA Ops:
  0.6 69.8 %shard_map.104 = (f32[8,32,128]{2,1,0:T(8,128)}, f32[3,8,32,128]{3,2,1,0:T(8,128)}) custom-call(f32[8]{0:T(128)} %sound.1, f32[8]{0:T(128)} %mass.1, f32[8,32,128]{2,1,0:T(8,128)} %dens_hbm.1, f32[3,8,32,128]{3,2,1,0:T(8,128)} %vel_hbm.1, s32[8,32,128]{2,1,0:T(8,128)} %lab_hbm.1, s32[32,128]{1,0:T(8,128)} %bitcast.2, f32[32,128]{1,0:T(8,128)} %bitcast.3, ...), custom_call_target="tpu_custom_call" | custom-call | tf_op jit(solution)/shard_map/pallas_call | solution.py:392
  70.4 1.6 %copy.13 = f32[8,32,128]{2,1,0:T(8,128)} copy(f32[8,32,128]{2,1,0:T(8,128)} %get-tuple-element.4) | data formatting | bytes 262144
  72.0 1.8 %copy.14 = f32[3,8,32,128]{3,2,1,0:T(8,128)} copy(f32[3,8,32,128]{3,2,1,0:T(8,128)} %get-tuple-element.5) | data formatting | bytes 786432
where the time goes:
time: 73.9 us; the launch traced here: 73.8 us
  Pallas kernels  69.8 us (94%)
  local copies, waits for them, and re-layouts  3.33 us (5%)
    pallas_call x1, Pallas kernels, shards(): pl.pallas_call(kernel, out_shape=(jax.ShapeDtypeStruct(field, F32), jax.S...  69.8 us
    unnamed x2, local copies, waits for them, and re-layouts  3.33 us

commit v1 on v0

--- a/solution.py
+++ b/solution.py
@@ -96,11 +96,11 @@
 
 
 def kernel(
-    sound, mass, dens_hbm, vel_hbm, lab_hbm, sidx, sval, small, large_hbm,
+    sound_hbm, mass_hbm, dens_hbm, vel_hbm, lab_hbm, sidx_hbm, sval_hbm, small_hbm, large_hbm,
     out_d, out_v,
-    send_buf, recv_buf, work, long_a, long_b, dens, vel, lab, large,
+    send_buf, recv_buf, work, long_a, long_b, sound, mass, dens, vel, lab, sidx, sval, small, large,
     base_v, coef_v, base_d, coef_d, corr, row_of, col_of,
-    send_sem, recv_sem, load_sem, out_sem,
+    send_sem, recv_sem, load_sem,
 ):
     gz = lax.axis_index("gz")
     gx = lax.axis_index("gx")
@@ -108,38 +108,53 @@
     me_b = lax.rem(gz, 16)
     me_a = z_hi * 4 + gx
 
+    b_x, b_y = lax.div(me_b, 4), lax.rem(me_b, 4)
+    far_b = sorted(
+        [(x, y) for x in range(4) for y in range(4) if x or y],
+        key=lambda o: -(min(o[0], 4 - o[0]) + min(o[1], 4 - o[1])),
+    )
+    peers = {
+        "A": [lax.rem(me_a + o, G) for o in sorted(range(1, G), key=lambda o: abs(o - 8))],
+        "B": [lax.rem(b_x + x, 4) * 4 + lax.rem(b_y + y, 4) for x, y in far_b],
+    }
+
     def device_of(group, peer):
         if group == "A":
             return (lax.div(peer, 4) * 16 + me_b, lax.rem(peer, 4))
         return (z_hi * 16 + peer, gx)
 
+    barrier = pltpu.get_barrier_semaphore()
+
+    for pair in zip(peers["A"], peers["B"]):
+        for group, peer in zip("AB", pair):
+            pl.semaphore_signal(
+                barrier, inc=1, device_id=device_of(group, peer), device_id_type=MESH
+            )
+
     loads = [
-        pltpu.make_async_copy(lab_hbm, lab, load_sem.at[0]),
-        pltpu.make_async_copy(dens_hbm, dens, load_sem.at[1]),
-        pltpu.make_async_copy(vel_hbm, vel, load_sem.at[2]),
-        pltpu.make_async_copy(large_hbm, large, load_sem.at[3]),
+        pltpu.make_async_copy(away, here, load_sem.at[i])
+        for i, (away, here) in enumerate(
+            (
+                (sound_hbm, sound),
+                (lab_hbm, lab),
+                (dens_hbm, dens),
+                (small_hbm, small),
+                (mass_hbm, mass),
+                (vel_hbm, vel),
+                (sidx_hbm, sidx),
+                (sval_hbm, sval),
+                (large_hbm, large),
+            )
+        )
     ]
     for load in loads:
         load.start()
 
-    barrier = pltpu.get_barrier_semaphore()
-
-    def greet(step, carry):
-        for group, me in (("A", me_a), ("B", me_b)):
-            peer = lax.rem(me + step, G)
-            pl.semaphore_signal(
-                barrier, inc=1, device_id=device_of(group, peer), device_id_type=MESH
-            )
-        return carry
-
-    lax.fori_loop(1, G, greet, 0)
-
     def send(which, group):
         me = me_a if group == "A" else me_b
         recv_buf[which, me] = send_buf[which, me]
 
-        def one(step, carry):
-            peer = lax.rem(me + step, G)
+        for peer in peers[group]:
             pltpu.make_async_remote_copy(
                 send_buf.at[which, peer],
                 recv_buf.at[which, me],
@@ -148,9 +163,6 @@
                 device_id=device_of(group, peer),
                 device_id_type=MESH,
             ).start()
-            return carry
-
-        lax.fori_loop(1, G, one, 0)
 
     def whole(which):
         return pltpu.make_async_copy(
@@ -168,9 +180,6 @@
             recv_buf.at[which, pl.ds(0, G - 1)],
             send_sem.at[which],
         ).wait()
-
-    r_small = (small[0], small[1])
-    d_small = (small[2], small[3])
 
     def put(which, value):
         send_buf[which] = value.reshape(G, 8, ROWS)
@@ -217,12 +226,14 @@
     def turned(which):
         return split(recv_buf[which].reshape(G * 8, ROWS).T)
 
+    for load in loads[:4]:
+        load.wait()
+    r_small = (small[0], small[1])
+    d_small = (small[2], small[3])
     speed_ref = sound[0]
     for tissue in range(1, LABELS):
         speed_ref = jnp.maximum(speed_ref, sound[tissue])
 
-    loads[0].wait()
-    loads[1].wait()
     classes = lab[...].reshape(ROWS, NY)
     speed = jnp.full((ROWS, NY), sound[0])
     for tissue in range(1, LABELS):
@@ -232,7 +243,8 @@
     pl.semaphore_wait(barrier, 2 * (G - 1))
     send(P_A, "A")
 
-    loads[2].wait()
+    for load in loads[4:8]:
+        load.wait()
     density_mass = jnp.full((ROWS, NY), mass[0])
     for tissue in range(1, LABELS):
         density_mass = jnp.where(classes == tissue, mass[tissue], density_mass)
@@ -308,7 +320,7 @@
 
     lax.fori_loop(0, SRC // NY // 2, add_some, 0)
 
-    loads[3].wait()
+    loads[8].wait()
     r_large = (large[0], large[1])
     d_large = (large[2], large[3])
 
@@ -330,7 +342,6 @@
     from_x_lines(UZ_A, product(turned(WZ_B), r_small, "nn"))
     send(UZ_A, "A")
 
-    stores = []
     for came, goes, a, back, sign in (
         (U0_A, VY_A, 2, d_small, -1),
         (UX_A, VX_A, 1, r_small, 1),
@@ -345,10 +356,7 @@
         else:
             put(goes, -product(d_small, halves, "nt"))
         send(goes, "A")
-        vel[a] = fresh.reshape(Z_LOC, X_LOC, NY)
-        store = pltpu.make_async_copy(vel.at[a], out_v.at[a], out_sem.at[a])
-        store.start()
-        stores.append(store)
+        out_v[a] = fresh.reshape(Z_LOC, X_LOC, NY)
 
     arrived(VY_A)
     part_y = product(r_small, split(to_x_lines(VY_A)), "nt")
@@ -372,40 +380,39 @@
 
     arrived(S_A)
     spread = product(turned(S_A), r_small, "nn")
-    dens[...] = (base_d[...] - coef_d[...] * spread).reshape(Z_LOC, X_LOC, NY)
-    store = pltpu.make_async_copy(dens, out_d, out_sem.at[3])
-    store.start()
-    stores.append(store)
+    out_d[...] = (base_d[...] - coef_d[...] * spread).reshape(Z_LOC, X_LOC, NY)
     for which in range(14):
         sent(which)
-    for store in stores:
-        store.wait()
 
 
 def shards(density, velocity, labels, sound_table, mass_table, source_index, source_values):
     small, large = tables()
     block = (G, 8, ROWS)
     vmem = pl.BlockSpec(memory_space=pltpu.VMEM)
-    smem = pl.BlockSpec(memory_space=pltpu.SMEM)
-    anyspace = pl.BlockSpec(memory_space=pl.ANY)
+    hbm = pl.BlockSpec(memory_space=pl.ANY)
     field = (Z_LOC, X_LOC, NY)
     return pl.pallas_call(
         kernel,
         out_shape=(
-            jax.ShapeDtypeStruct(field, F32),
-            jax.ShapeDtypeStruct((3,) + field, F32),
+            pltpu.VMEM(field, F32),
+            pltpu.VMEM((3,) + field, F32),
         ),
-        in_specs=[smem, smem, anyspace, anyspace, anyspace, vmem, vmem, vmem, anyspace],
-        out_specs=(anyspace, anyspace),
+        in_specs=[hbm] * 9,
+        out_specs=(vmem, vmem),
         scratch_shapes=[
             pltpu.VMEM((14,) + block, F32),
             pltpu.VMEM((14,) + block, F32),
             pltpu.VMEM((ROWS, NY), F32),
             pltpu.VMEM((64, NZ), F32),
             pltpu.VMEM((64, NZ), F32),
+            pltpu.SMEM((LABELS,), F32),
+            pltpu.SMEM((LABELS,), F32),
             pltpu.VMEM(field, F32),
             pltpu.VMEM((3,) + field, F32),
             pltpu.VMEM(field, jnp.int32),
+            pltpu.VMEM((SRC // NY, NY), jnp.int32),
+            pltpu.VMEM((SRC // NY, NY), F32),
+            pltpu.VMEM((4, NX, NX), BF16),
             pltpu.VMEM((4, NZ, NZ), BF16),
             pltpu.VMEM((3, ROWS, NY), F32),
             pltpu.VMEM((3, ROWS, NY), F32),
@@ -416,8 +423,7 @@
             pltpu.VMEM((SRC // NY, NY), jnp.int32),
             pltpu.SemaphoreType.DMA((14,)),
             pltpu.SemaphoreType.DMA((14,)),
-            pltpu.SemaphoreType.DMA((4,)),
-            pltpu.SemaphoreType.DMA((4,)),
+            pltpu.SemaphoreType.DMA((9,)),
         ],
         compiler_params=pltpu.CompilerParams(collective_id=0, has_side_effects=True),
     )(

time: 73.9 us -> 65.5 us (0.89)
  Pallas kernels: 69.8 us -> 63.3 us
  local copies, waits for them, and re-layouts: 3.33 us -> 1.4 us
    pallas_call x1, Pallas kernels: 69.8 us -> 63.3 us  [shards(): pl.pallas_call(kernel, out_shape=(pltpu.VMEM(field, F32), pltpu.VMEM((3,)...]
    unnamed x2, local copies, waits for them, and re-layouts: 3.33 us -> 1.4 us
where the time goes in v1:
time: 65.5 us; the launch traced here: 65.4 us
  Pallas kernels  63.3 us (97%)
  local copies, waits for them, and re-layouts  1.4 us (2%)
    pallas_call x1, Pallas kernels, shards(): pl.pallas_call(kernel, out_shape=(pltpu.VMEM(field, F32), pltpu.VMEM((3,)...  63.3 us
    unnamed x2, local copies, waits for them, and re-layouts  1.4 us

profile of v1, /device:TPU:1, one launch (start us, length us, event | category | flops | bytes accessed | tf_op | source)
XLA Modules:
  0.0 65.4 jit_solution(8054763904181350667)
XLA Ops:
  0.6 63.3 %shard_map.104 = (f32[8,32,128]{2,1,0:T(8,128)S(1)}, f32[3,8,32,128]{3,2,1,0:T(8,128)S(1)}) custom-call(f32[8]{0:T(128)} %sound_hbm.1, f32[8]{0:T(128)} %mass_hbm.1, f32[8,32,128]{2,1,0:T(8,128)} %dens_hbm.1, f32[3,8,32,128]{3,2,1,0:T(8,128)} %vel_hbm.1, s32[8,32,128]{2,1,0:T(8,128)} %lab_hbm.1, s32[32,128]{1,0:T(8,128)} %bitcast.2, f32[32,128]{1,0:T(8,128)} %bitcast.3, ...), custom_call_target="tpu_custom_call" | custom-call | tf_op jit(solution)/shard_map/pallas_call | solution.py:394
  64.0 0.7 %copy.13 = f32[8,32,128]{2,1,0:T(8,128)} copy(f32[8,32,128]{2,1,0:T(8,128)S(1)} %get-tuple-element.2) | data formatting | bytes 262144
  64.6 0.7 %copy.14 = f32[3,8,32,128]{3,2,1,0:T(8,128)} copy(f32[3,8,32,128]{3,2,1,0:T(8,128)S(1)} %get-tuple-element.3) | data formatting | bytes 786432

commit v2 on v1

v2 whole, which is shorter than its diff:
```python
import math

import jax
import jax.numpy as jnp
import numpy as np
from jax import lax
from jax.experimental import pallas as pl
from jax.experimental.pallas import tpu as pltpu
from jax.sharding import PartitionSpec as P

NZ = 512
NX = 128
NY = 128
LABELS = 8
PML_W = 20
SRC = 4096
DT = 0.3
ABSORB = 2.0
CHIPS = 128
WIDE = CHIPS * 8
Z_LOC = 8
X_LOC = 32
ROWS = Z_LOC * X_LOC
MESH = pl.DeviceIdType.MESH
F32 = jnp.float32
BF16 = jnp.bfloat16

P_S, U0_S, UX_S, UZ_S, VY_S, VX_S, VZ_S, E_S = range(8)
P_C, X_C, YZ_C = range(3)
V0_I, VX_I, E_I = range(3)


def basis(n):
    j = np.arange(n)
    f = np.concatenate([np.arange(n // 2 + 1), np.arange(1, n // 2)])
    is_sin = (np.arange(n) > n // 2)[:, None]
    scale = np.where((f == 0) | (f == n // 2), math.sqrt(1.0 / n), math.sqrt(2.0 / n))[:, None]
    k = (2.0 * math.pi / n * f)[:, None]
    phase = 2.0 * math.pi / n * ((f[:, None] * j[None, :]) % n)
    half = 2.0 * math.pi / (2 * n) * ((f[:, None] * (2 * j[None, :] + 1)) % (2 * n))
    forward = np.where(is_sin, np.sin(phase), np.cos(phase)) * scale
    slope = np.where(is_sin, k * np.cos(half), -k * np.sin(half)) * scale
    return forward, slope


def parts(table):
    table = table.astype(np.float32)
    high = table.astype(jnp.bfloat16)
    low = (table - high.astype(np.float32)).astype(jnp.bfloat16)
    return [high, low]


def tables():
    r, d = basis(NX)
    lane = np.arange(NX)
    x_of = [((lane % 64) // 32 * 2 + (lane // 64 + core) % 2) * X_LOC + lane % 32 for core in range(2)]
    small = np.stack([np.stack(parts(r[:, x]) + parts(d[:, x])) for x in [lane] + x_of])
    r, d = basis(NZ)
    row = np.arange(NZ)
    z = (row % 64) * Z_LOC + row // 64
    large = np.stack(parts(r[:, z]) + parts(d[:, z]))
    return small, large


def split(x):
    high = x.astype(BF16)
    return high, (x - high.astype(F32)).astype(BF16)


def product(a, b, dims):
    contract = (((1,), (0 if dims == "nn" else 1,)), ((), ()))
    a, b = (x() if callable(x) else x for x in (a, b))

    def dot(u, v):
        return lax.dot_general(u, v, contract, preferred_element_type=F32)

    return dot(a[0], b[0]) + dot(a[1], b[0]) + dot(a[0], b[1])


def interleave(u, v):
    even = lax.broadcasted_iota(jnp.int32, u.shape, 1) % 64 < 32
    return jnp.where(even, u, pltpu.roll(v, 32, 1)), jnp.where(even, pltpu.roll(u, 96, 1), v)


def low_half(shape):
    return lax.broadcasted_iota(jnp.int32, shape, 1) < 64


def both(u):
    low = low_half(u.shape)
    other = pltpu.roll(u, 64, 1)
    return jnp.where(low, u, other), jnp.where(low, other, u)


def kernel(
    sound_hbm, mass_hbm, dens_hbm, vel_hbm, lab_hbm, sidx_hbm, sval_hbm, small_hbm, large_hbm,
    out_d, out_v,
    send_buf, recv_buf, half_send, half_recv, back_send, back_recv,
    sound, mass, dens, vel, lab, sidx, sval, flat, mixed, large, turned_large,
    base_v, coef_v, base_d, coef_d, corr, row_of, col_of,
    send_sem, recv_sem, half_sem, half_got, back_sem, back_got, load_sem,
):
    gz = lax.axis_index("gz")
    gx = lax.axis_index("gx")
    core = lax.rem(gx, 2)
    me = gz * 2 + lax.div(gx, 2)
    partner = (gz, gx + 1 - 2 * core)

    loads = [
        pltpu.make_async_copy(away, here, load_sem.at[i])
        for i, (away, here) in enumerate(
            (
                (sound_hbm, sound),
                (lab_hbm, lab),
                (dens_hbm, dens),
                (small_hbm.at[0], flat),
                (mass_hbm, mass),
                (vel_hbm, vel),
                (sidx_hbm, sidx),
                (sval_hbm, sval),
                (small_hbm.at[1 + core], mixed),
                (large_hbm, large),
            )
        )
    ]
    for load in loads:
        load.start()

    own_low = lax.div(gx, 2)
    neighbour = (gz, gx + 2 - 4 * own_low)

    def each_peer(visit):
        def place(at, carry):
            for low in range(2):
                visit(at, low, (at, 2 * low + core))
            return carry

        def pair(step, carry):
            place(lax.rem(gz + 32 + step, 64), 0)
            place(lax.rem(gz + 32 - step, 64), 0)
            return carry

        place(lax.rem(gz + 32, 64), 0)
        lax.fori_loop(1, 32, pair, 0)
        visit(gz, 1 - own_low, neighbour)

    barrier = pltpu.get_barrier_semaphore()

    def greet(at, low, device):
        pl.semaphore_signal(barrier, inc=1, device_id=device, device_id_type=MESH)

    each_peer(greet)
    pl.semaphore_signal(barrier, inc=1, device_id=partner, device_id_type=MESH)

    def send(which):
        own = pl.ds(pl.multiple_of(me * 8, 8), 2)
        recv_buf[which, own, :] = send_buf[which, own, :]

        def one(at, low, device):
            pltpu.make_async_remote_copy(
                send_buf.at[which, pl.ds(pl.multiple_of(at * 16 + low * 8, 8), 2)],
                recv_buf.at[which, own],
                send_sem.at[which],
                recv_sem.at[which],
                device_id=device,
                device_id_type=MESH,
            ).start()

        each_peer(one)

    some = pl.ds(0, 2 * (CHIPS - 1))

    def arrived(which):
        pltpu.make_async_copy(
            send_buf.at[which, some], recv_buf.at[which, some], recv_sem.at[which]
        ).wait()

    def sent(which):
        pltpu.make_async_copy(
            send_buf.at[which, some], recv_buf.at[which, some], send_sem.at[which]
        ).wait()

    def put(which, value):
        for tile in range(2):
            send_buf[which, pl.ds(tile, CHIPS, stride=8), :] = value[:, tile * 128 : tile * 128 + 128]

    def turned(which):
        tiles = [recv_buf[which, pl.ds(tile, CHIPS, stride=8), :].T for tile in range(2)]
        return split(jnp.concatenate(tiles, axis=0))

    def get_slab(which):
        blocks = []
        for tile in range(2):
            near = [recv_buf[which, pl.ds(tile + 8 * low, 64, stride=16), :] for low in range(2)]
            b0, b1 = interleave(*near)
            q0, q2 = both(b0)
            q1, q3 = both(b1)
            blocks += [q0, q1, q2, q3]
        return split(jnp.concatenate(blocks, axis=0))

    def put_slab(which, value):
        low = low_half((64, 128))
        for tile in range(2):
            q = [value[(tile * 4 + i) * 64 : (tile * 4 + i) * 64 + 64] for i in range(4)]
            near = interleave(jnp.where(low, q[0], q[2]), jnp.where(low, q[1], q[3]))
            for at in range(2):
                send_buf[which, pl.ds(tile + 8 * at, 64, stride=16), :] = near[at]

    low = low_half((128, 128))

    def give_half(which, value):
        for half in range(2):
            top = value[half * 256 : half * 256 + 128]
            bottom = value[half * 256 + 128 : half * 256 + 256]
            half_send[which, half] = jnp.where(low, top, bottom)
        copy = pltpu.make_async_remote_copy(
            half_send.at[which, 1 - core],
            half_recv.at[which],
            half_sem.at[which],
            half_got.at[which],
            device_id=partner,
            device_id_type=MESH,
        )
        copy.start()
        return copy

    def take_half(which, copy):
        copy.wait_recv()
        mine = half_send[which, core]
        other = half_recv[which]
        top = jnp.where(low, mine, pltpu.roll(other, 64, 1))
        bottom = jnp.where(low, pltpu.roll(mine, 64, 1), other)
        return split(jnp.concatenate([top, bottom], axis=0))

    def give_back(which, value):
        top, bottom = value[:128], value[128:]
        back_recv[which, core] = jnp.where(low, top, pltpu.roll(bottom, 64, 1))
        back_send[which] = jnp.where(low, pltpu.roll(top, 64, 1), bottom)
        copy = pltpu.make_async_remote_copy(
            back_send.at[which],
            back_recv.at[which, core],
            back_sem.at[which],
            back_got.at[which],
            device_id=partner,
            device_id_type=MESH,
        )
        copy.start()
        return copy

    def take_back(which, copy):
        copy.wait_recv()
        return split(jnp.concatenate(both(back_recv[which, 0]) + both(back_recv[which, 1]), axis=0))

    for load in loads[:4]:
        load.wait()
    def r_flat():
        return flat[0], flat[1]

    def d_flat():
        return flat[2], flat[3]

    speed_ref = sound[0]
    for tissue in range(1, LABELS):
        speed_ref = jnp.maximum(speed_ref, sound[tissue])

    classes = lab[...].reshape(ROWS, NY)
    speed = jnp.full((ROWS, NY), sound[0])
    for tissue in range(1, LABELS):
        speed = jnp.where(classes == tissue, sound[tissue], speed)
    pressure = speed * speed * dens[...].reshape(ROWS, NY)
    put(P_S, product(r_flat, split(pressure), "nt"))
    pl.semaphore_wait(barrier, CHIPS)
    send(P_S)

    for load in loads[4:8]:
        load.wait()
    density_mass = jnp.full((ROWS, NY), mass[0])
    for tissue in range(1, LABELS):
        density_mass = jnp.where(classes == tissue, mass[tissue], density_mass)
    row = lax.broadcasted_iota(jnp.int32, (ROWS, NY), 0)
    col = lax.broadcasted_iota(jnp.int32, (ROWS, NY), 1)

    def damping(position, length):
        coordinate = position.astype(F32)
        depth = jnp.maximum(
            jnp.maximum(PML_W - coordinate, coordinate - (length - 1 - PML_W)), 0.0
        ) / PML_W
        square = depth * depth
        return jnp.exp(-ABSORB * speed_ref * (square * square) * DT * 0.5)

    damp = (
        damping(gz * Z_LOC + row // X_LOC, NZ),
        damping(gx * X_LOC + row % X_LOC, NX),
        damping(col, NY),
    )
    over_mass = DT / density_mass
    for a in range(3):
        base_v[a] = damp[a] * (damp[a] * vel[a].reshape(ROWS, NY))
        coef_v[a] = damp[a] * over_mass
    damp_all = damp[0] * damp[1] * damp[2]
    base_d[...] = damp_all * (damp_all * dens[...].reshape(ROWS, NY))
    coef_d[...] = damp_all * (DT * density_mass)

    line = lax.broadcasted_iota(jnp.int32, (256, NX), 0)
    index_x = lax.broadcasted_iota(jnp.int32, (256, NX), 1)

    def wave(index, length):
        folded = jnp.where(index <= length // 2, index, index - length // 2)
        return folded.astype(F32) * (2.0 * math.pi / length)

    wz = wave(core * 256 + line, NZ)
    wx = wave(index_x, NX)
    wy = wave(jnp.full((256, NX), me, jnp.int32), NY)
    angle = speed_ref * jnp.sqrt(wz * wz + wx * wx + wy * wy) * (DT / 2.0)
    at_zero = angle == 0.0
    safe = jnp.where(at_zero, 1.0, angle)
    corr[...] = jnp.where(at_zero, 1.0, jnp.sin(safe) / safe)

    for load in loads[8:]:
        load.wait()
    for table in range(4):
        turned_large[table] = large[table].T
    def r_mixed():
        return mixed[0], mixed[1]

    def d_mixed():
        return mixed[2], mixed[3]

    def r_large():
        return large[0], large[1]

    def d_large():
        return large[2], large[3]

    def r_turned():
        return turned_large[0], turned_large[1]

    def d_turned():
        return turned_large[2], turned_large[3]

    copies = []

    arrived(P_S)
    copy = give_half(P_C, product(r_large, get_slab(P_S), "nn"))
    copies.append(copy)
    spectrum = product(take_half(P_C, copy), r_mixed, "nt")
    spectrum = split(spectrum * corr[...])
    back_0 = give_back(V0_I, product(spectrum, r_mixed, "nn"))
    back_x = give_back(VX_I, product(spectrum, d_mixed, "nn"))
    copies += [back_0, back_x]
    field = take_back(V0_I, back_0)
    put_slab(U0_S, product(r_turned, field, "nn"))
    send(U0_S)
    put_slab(UX_S, product(r_turned, take_back(VX_I, back_x), "nn"))
    send(UX_S)
    put_slab(UZ_S, product(d_turned, field, "nn"))
    send(UZ_S)

    where = sidx[...]
    plane = NX * NY
    z_off = where // plane - gz * Z_LOC
    remain = where % plane
    x_off = remain // NY - gx * X_LOC
    inside = (z_off >= 0) & (z_off < Z_LOC) & (x_off >= 0) & (x_off < X_LOC)
    row_of[...] = jnp.where(inside, z_off * X_LOC + x_off, -1)
    col_of[...] = remain % NY

    def add_some(step, carry):
        picks = []
        highs = []
        lows = []
        for part in range(2):
            at = pl.ds(step * 2 + part, 1)
            picks.append(jnp.where(row == row_of[at, :], 1.0, 0.0).astype(BF16))
            amount = jnp.where(row[:NY] == col_of[at, :], sval[at, :], 0.0)
            high, low = split(amount)
            highs.append(high)
            lows.append(low)
        pick = jnp.concatenate(picks, axis=1)
        contract = (((1,), (1,)), ((), ()))
        high = lax.dot_general(pick, jnp.concatenate(highs, axis=1), contract, preferred_element_type=F32)
        low = lax.dot_general(pick, jnp.concatenate(lows, axis=1), contract, preferred_element_type=F32)
        base_d[...] += high + low
        return carry

    lax.fori_loop(0, SRC // NY // 2, add_some, 0)

    for came, goes, a, back, sign in (
        (U0_S, VY_S, 2, d_flat, -1),
        (UX_S, VX_S, 1, r_flat, 1),
        (UZ_S, VZ_S, 0, r_flat, 1),
    ):
        arrived(came)
        slope = product(turned(came), back, "nn")
        fresh = base_v[a] - coef_v[a] * slope
        halves = split(fresh)
        if sign > 0:
            put(goes, product(r_flat, halves, "nt"))
        else:
            put(goes, -product(d_flat, halves, "nt"))
        send(goes)
        out_v[a] = fresh.reshape(Z_LOC, X_LOC, NY)

    arrived(VY_S)
    part_yz = product(r_large, get_slab(VY_S), "nn")
    arrived(VX_S)
    copy_x = give_half(X_C, product(r_large, get_slab(VX_S), "nn"))
    spectrum = product(take_half(X_C, copy_x), d_mixed, "nt")
    arrived(VZ_S)
    copy_yz = give_half(YZ_C, part_yz - product(d_large, get_slab(VZ_S), "nn"))
    spectrum = product(take_half(YZ_C, copy_yz), r_mixed, "nt") - spectrum
    back_e = give_back(E_I, product(split(spectrum * corr[...]), r_mixed, "nn"))
    copies += [copy_x, copy_yz, back_e]
    put_slab(E_S, product(r_turned, take_back(E_I, back_e), "nn"))
    send(E_S)

    arrived(E_S)
    spread = product(turned(E_S), r_flat, "nn")
    out_d[...] = (base_d[...] - coef_d[...] * spread).reshape(Z_LOC, X_LOC, NY)
    for which in range(8):
        sent(which)
    for copy in copies:
        copy.wait_send()


def shards(density, velocity, labels, sound_table, mass_table, source_index, source_values):
    small, large = tables()
    vmem = pl.BlockSpec(memory_space=pltpu.VMEM)
    hbm = pl.BlockSpec(memory_space=pl.ANY)
    field = (Z_LOC, X_LOC, NY)
    return pl.pallas_call(
        kernel,
        out_shape=(
            pltpu.VMEM(field, F32),
            pltpu.VMEM((3,) + field, F32),
        ),
        in_specs=[hbm] * 9,
        out_specs=(vmem, vmem),
        scratch_shapes=[
            pltpu.VMEM((8, WIDE, 128), F32),
            pltpu.VMEM((8, WIDE, 128), F32),
            pltpu.VMEM((3, 2, 128, 128), F32),
            pltpu.VMEM((3, 128, 128), F32),
            pltpu.VMEM((3, 128, 128), F32),
            pltpu.VMEM((3, 2, 128, 128), F32),
            pltpu.SMEM((LABELS,), F32),
            pltpu.SMEM((LABELS,), F32),
            pltpu.VMEM(field, F32),
            pltpu.VMEM((3,) + field, F32),
            pltpu.VMEM(field, jnp.int32),
            pltpu.VMEM((SRC // NY, NY), jnp.int32),
            pltpu.VMEM((SRC // NY, NY), F32),
            pltpu.VMEM((4, NX, NX), BF16),
            pltpu.VMEM((4, NX, NX), BF16),
            pltpu.VMEM((4, NZ, NZ), BF16),
            pltpu.VMEM((4, NZ, NZ), BF16),
            pltpu.VMEM((3, ROWS, NY), F32),
            pltpu.VMEM((3, ROWS, NY), F32),
            pltpu.VMEM((ROWS, NY), F32),
            pltpu.VMEM((ROWS, NY), F32),
            pltpu.VMEM((256, NX), F32),
            pltpu.VMEM((SRC // NY, NY), jnp.int32),
            pltpu.VMEM((SRC // NY, NY), jnp.int32),
            pltpu.SemaphoreType.DMA((8,)),
            pltpu.SemaphoreType.DMA((8,)),
            pltpu.SemaphoreType.DMA((3,)),
            pltpu.SemaphoreType.DMA((3,)),
            pltpu.SemaphoreType.DMA((3,)),
            pltpu.SemaphoreType.DMA((3,)),
            pltpu.SemaphoreType.DMA((10,)),
        ],
        compiler_params=pltpu.CompilerParams(collective_id=0, has_side_effects=True),
    )(
        sound_table,
        mass_table,
        density,
        velocity,
        labels,
        source_index.reshape(SRC // NY, NY),
        source_values[0].reshape(SRC // NY, NY),
        jnp.asarray(small),
        jnp.asarray(large),
    )


def solution(mesh):
    in_specs = (
        P("gz", "gx", None),
        P(None, "gz", "gx", None),
        P("gz", "gx", None),
        P(),
        P(),
        P(),
        P(),
    )
    out_specs = (P("gz", "gx", None), P(None, "gz", "gx", None))
    return jax.shard_map(shards, mesh=mesh, in_specs=in_specs, out_specs=out_specs, check_vma=False)
```

time: 65.5 us -> 64.6 us (0.986)
  Pallas kernels: 63.3 us -> 62.5 us
    pallas_call x1, Pallas kernels: 63.3 us -> 62.5 us  [shards(): pl.pallas_call(kernel, out_shape=(pltpu.VMEM(field, F32), pltpu.VMEM((3,)...]
where the time goes in v2:
time: 64.6 us; the launch traced here: 64.5 us
  Pallas kernels  62.5 us (97%)
  local copies, waits for them, and re-layouts  1.4 us (2%)
    pallas_call x1, Pallas kernels, shards(): pl.pallas_call(kernel, out_shape=(pltpu.VMEM(field, F32), pltpu.VMEM((3,)...  62.5 us
    unnamed x2, local copies, waits for them, and re-layouts  1.4 us

profile of v2, /device:TPU:1, one launch (start us, length us, event | category | flops | bytes accessed | tf_op | source)
XLA Modules:
  0.0 64.5 jit_solution(1989275451012831803)
XLA Ops:
  0.6 62.5 %shard_map.104 = (f32[8,32,128]{2,1,0:T(8,128)S(1)}, f32[3,8,32,128]{3,2,1,0:T(8,128)S(1)}) custom-call(f32[8]{0:T(128)} %sound_hbm.1, f32[8]{0:T(128)} %mass_hbm.1, f32[8,32,128]{2,1,0:T(8,128)} %dens_hbm.1, f32[3,8,32,128]{3,2,1,0:T(8,128)} %vel_hbm.1, s32[8,32,128]{2,1,0:T(8,128)} %lab_hbm.1, s32[32,128]{1,0:T(8,128)} %bitcast.2, f32[32,128]{1,0:T(8,128)} %bitcast.3, ...), custom_call_target="tpu_custom_call" | custom-call | tf_op jit(solution)/shard_map/pallas_call | solution.py:431
  63.1 0.7 %copy.13 = f32[8,32,128]{2,1,0:T(8,128)} copy(f32[8,32,128]{2,1,0:T(8,128)S(1)} %get-tuple-element.2) | data formatting | bytes 262144
  63.8 0.7 %copy.14 = f32[3,8,32,128]{3,2,1,0:T(8,128)} copy(f32[3,8,32,128]{3,2,1,0:T(8,128)S(1)} %get-tuple-element.3) | data formatting | bytes 786432

commit v3 on v2

--- a/solution.py
+++ b/solution.py
@@ -56,9 +56,15 @@
     x_of = [((lane % 64) // 32 * 2 + (lane // 64 + core) % 2) * X_LOC + lane % 32 for core in range(2)]
     small = np.stack([np.stack(parts(r[:, x]) + parts(d[:, x])) for x in [lane] + x_of])
     r, d = basis(NZ)
-    row = np.arange(NZ)
-    z = (row % 64) * Z_LOC + row // 64
-    large = np.stack(parts(r[:, z]) + parts(d[:, z]))
+    frequency = np.concatenate([np.arange(NZ // 2 + 1), np.arange(1, NZ // 2)])
+    row = np.arange(NZ // 2)
+    z = (row % 32) * Z_LOC + row // 32
+    large = np.stack(
+        [
+            np.stack(parts(r[frequency % 2 == odd][:, z]) + parts(d[frequency % 2 == odd][:, z]))
+            for odd in range(2)
+        ]
+    )
     return small, large
 
 
@@ -188,31 +194,52 @@
         tiles = [recv_buf[which, pl.ds(tile, CHIPS, stride=8), :].T for tile in range(2)]
         return split(jnp.concatenate(tiles, axis=0))
 
+    low = low_half((128, 128))
+    low_32 = low_half((32, 128))
+
+    def stacked(blocks):
+        value = jnp.concatenate(blocks, axis=0)
+        high = value.astype(BF16).astype(F32)
+        return jnp.where(low_half(value.shape), value, value - high).astype(BF16)
+
+    def long_product(tables, value):
+        def dot(table):
+            return jnp.dot(table, value, preferred_element_type=F32)
+
+        return dot(tables[0]) + dot(tables[1])
+
+    def combine(u, v, mask):
+        return jnp.where(mask, u, v) + pltpu.roll(jnp.where(mask, v, u), 64, 1)
+
     def get_slab(which):
-        blocks = []
+        folds = ([], [])
         for tile in range(2):
-            near = [recv_buf[which, pl.ds(tile + 8 * low, 64, stride=16), :] for low in range(2)]
-            b0, b1 = interleave(*near)
-            q0, q2 = both(b0)
-            q1, q3 = both(b1)
-            blocks += [q0, q1, q2, q3]
-        return split(jnp.concatenate(blocks, axis=0))
-
-    def put_slab(which, value):
-        low = low_half((64, 128))
+            near = [recv_buf[which, pl.ds(tile + 8 * at, 64, stride=16), :] for at in range(2)]
+            for blocks, sign in zip(folds, (1, -1)):
+                b0, b1 = interleave(*[a[:32] + sign * a[32:] for a in near])
+                q0, q2 = both(b0)
+                q1, q3 = both(b1)
+                blocks += [q0, q1, q2, q3]
+        return [stacked(blocks) for blocks in folds]
+
+    def put_slab(which, folds):
         for tile in range(2):
-            q = [value[(tile * 4 + i) * 64 : (tile * 4 + i) * 64 + 64] for i in range(4)]
-            near = interleave(jnp.where(low, q[0], q[2]), jnp.where(low, q[1], q[3]))
+            ends = []
+            for value in folds:
+                q = [value[(tile * 4 + i) * 32 : (tile * 4 + i) * 32 + 32] for i in range(4)]
+                ends.append(interleave(combine(q[0], q[2], low_32), combine(q[1], q[3], low_32)))
             for at in range(2):
-                send_buf[which, pl.ds(tile + 8 * at, 64, stride=16), :] = near[at]
-
-    low = low_half((128, 128))
+                first = tile + 8 * at
+                send_buf[which, pl.ds(first, 32, stride=16), :] = ends[0][at] + ends[1][at]
+                send_buf[which, pl.ds(first + 512, 32, stride=16), :] = ends[0][at] - ends[1][at]
+
+    def along_z(table, folds):
+        return [long_product((table[h, 0], table[h, 1]), folds[h]) for h in range(2)]
+
 
     def give_half(which, value):
         for half in range(2):
-            top = value[half * 256 : half * 256 + 128]
-            bottom = value[half * 256 + 128 : half * 256 + 256]
-            half_send[which, half] = jnp.where(low, top, bottom)
+            half_send[which, half] = combine(value[half][:128], value[half][128:], low)
         copy = pltpu.make_async_remote_copy(
             half_send.at[which, 1 - core],
             half_recv.at[which],
@@ -249,7 +276,7 @@
 
     def take_back(which, copy):
         copy.wait_recv()
-        return split(jnp.concatenate(both(back_recv[which, 0]) + both(back_recv[which, 1]), axis=0))
+        return [stacked(both(back_recv[which, half])) for half in range(2)]
 
     for load in loads[:4]:
         load.wait()
@@ -308,7 +335,8 @@
         folded = jnp.where(index <= length // 2, index, index - length // 2)
         return folded.astype(F32) * (2.0 * math.pi / length)
 
-    wz = wave(core * 256 + line, NZ)
+    folded = jnp.where(line <= 128 - core, line, line - 128)
+    wz = (2 * folded + core).astype(F32) * (2.0 * math.pi / NZ)
     wx = wave(index_x, NX)
     wy = wave(jnp.full((256, NX), me, jnp.int32), NY)
     angle = speed_ref * jnp.sqrt(wz * wz + wx * wx + wy * wy) * (DT / 2.0)
@@ -318,30 +346,22 @@
 
     for load in loads[8:]:
         load.wait()
-    for table in range(4):
-        turned_large[table] = large[table].T
+    for half in range(2):
+        for table in range(4):
+            turned_large[half, table] = large[half, table].T
+    r_large, d_large = large.at[:, 0:2], large.at[:, 2:4]
+    r_turned, d_turned = turned_large.at[:, 0:2], turned_large.at[:, 2:4]
+
     def r_mixed():
         return mixed[0], mixed[1]
 
     def d_mixed():
         return mixed[2], mixed[3]
 
-    def r_large():
-        return large[0], large[1]
-
-    def d_large():
-        return large[2], large[3]
-
-    def r_turned():
-        return turned_large[0], turned_large[1]
-
-    def d_turned():
-        return turned_large[2], turned_large[3]
-
     copies = []
 
     arrived(P_S)
-    copy = give_half(P_C, product(r_large, get_slab(P_S), "nn"))
+    copy = give_half(P_C, along_z(r_large, get_slab(P_S)))
     copies.append(copy)
     spectrum = product(take_half(P_C, copy), r_mixed, "nt")
     spectrum = split(spectrum * corr[...])
@@ -349,11 +369,11 @@
     back_x = give_back(VX_I, product(spectrum, d_mixed, "nn"))
     copies += [back_0, back_x]
     field = take_back(V0_I, back_0)
-    put_slab(U0_S, product(r_turned, field, "nn"))
+    put_slab(U0_S, along_z(r_turned, field))
     send(U0_S)
-    put_slab(UX_S, product(r_turned, take_back(VX_I, back_x), "nn"))
+    put_slab(UX_S, along_z(r_turned, take_back(VX_I, back_x)))
     send(UX_S)
-    put_slab(UZ_S, product(d_turned, field, "nn"))
+    put_slab(UZ_S, along_z(d_turned, field))
     send(UZ_S)
 
     where = sidx[...]
@@ -402,16 +422,18 @@
         out_v[a] = fresh.reshape(Z_LOC, X_LOC, NY)
 
     arrived(VY_S)
-    part_yz = product(r_large, get_slab(VY_S), "nn")
+    part_yz = along_z(r_large, get_slab(VY_S))
     arrived(VX_S)
-    copy_x = give_half(X_C, product(r_large, get_slab(VX_S), "nn"))
+    copy_x = give_half(X_C, along_z(r_large, get_slab(VX_S)))
     spectrum = product(take_half(X_C, copy_x), d_mixed, "nt")
     arrived(VZ_S)
-    copy_yz = give_half(YZ_C, part_yz - product(d_large, get_slab(VZ_S), "nn"))
+    copy_yz = give_half(
+        YZ_C, [y - z for y, z in zip(part_yz, along_z(d_large, get_slab(VZ_S)))]
+    )
     spectrum = product(take_half(YZ_C, copy_yz), r_mixed, "nt") - spectrum
     back_e = give_back(E_I, product(split(spectrum * corr[...]), r_mixed, "nn"))
     copies += [copy_x, copy_yz, back_e]
-    put_slab(E_S, product(r_turned, take_back(E_I, back_e), "nn"))
+    put_slab(E_S, along_z(r_turned, take_back(E_I, back_e)))
     send(E_S)
 
     arrived(E_S)
@@ -452,8 +474,8 @@
             pltpu.VMEM((SRC // NY, NY), F32),
             pltpu.VMEM((4, NX, NX), BF16),
             pltpu.VMEM((4, NX, NX), BF16),
-            pltpu.VMEM((4, NZ, NZ), BF16),
-            pltpu.VMEM((4, NZ, NZ), BF16),
+            pltpu.VMEM((2, 4, NZ // 2, NZ // 2), BF16),
+            pltpu.VMEM((2, 4, NZ // 2, NZ // 2), BF16),
             pltpu.VMEM((3, ROWS, NY), F32),
             pltpu.VMEM((3, ROWS, NY), F32),
             pltpu.VMEM((ROWS, NY), F32),

time: 64.6 us -> 62.4 us (0.966)
  Pallas kernels: 62.5 us -> 60.2 us
    pallas_call x1, Pallas kernels: 62.5 us -> 60.2 us  [shards(): pl.pallas_call(kernel, out_shape=(pltpu.VMEM(field, F32), pltpu.VMEM((3,)...]
where the time goes in v3:
time: 62.4 us; the launch traced here: 62.3 us
  Pallas kernels  60.2 us (96%)
  local copies, waits for them, and re-layouts  1.4 us (2%)
  between operations  0.64 us (1%)
    pallas_call x1, Pallas kernels, shards(): pl.pallas_call(kernel, out_shape=(pltpu.VMEM(field, F32), pltpu.VMEM((3,)...  60.2 us
    unnamed x2, local copies, waits for them, and re-layouts  1.4 us

profile of v3, /device:TPU:1, one launch (start us, length us, event | category | flops | bytes accessed | tf_op | source)
XLA Modules:
  0.0 62.3 jit_solution(3366522568221163313)
XLA Ops:
  0.6 60.2 %shard_map.104 = (f32[8,32,128]{2,1,0:T(8,128)S(1)}, f32[3,8,32,128]{3,2,1,0:T(8,128)S(1)}) custom-call(f32[8]{0:T(128)} %sound_hbm.1, f32[8]{0:T(128)} %mass_hbm.1, f32[8,32,128]{2,1,0:T(8,128)} %dens_hbm.1, f32[3,8,32,128]{3,2,1,0:T(8,128)} %vel_hbm.1, s32[8,32,128]{2,1,0:T(8,128)} %lab_hbm.1, s32[32,128]{1,0:T(8,128)} %bitcast.2, f32[32,128]{1,0:T(8,128)} %bitcast.3, ...), custom_call_target="tpu_custom_call" | custom-call | tf_op jit(solution)/shard_map/pallas_call | solution.py:453
  60.9 0.7 %copy.13 = f32[8,32,128]{2,1,0:T(8,128)} copy(f32[8,32,128]{2,1,0:T(8,128)S(1)} %get-tuple-element.2) | data formatting | bytes 262144
  61.5 0.7 %copy.14 = f32[3,8,32,128]{3,2,1,0:T(8,128)} copy(f32[3,8,32,128]{3,2,1,0:T(8,128)S(1)} %get-tuple-element.3) | data formatting | bytes 786432

commit v4 on v3

--- a/solution.py
+++ b/solution.py
@@ -101,7 +101,7 @@
 def kernel(
     sound_hbm, mass_hbm, dens_hbm, vel_hbm, lab_hbm, sidx_hbm, sval_hbm, small_hbm, large_hbm,
     out_d, out_v,
-    send_buf, recv_buf, half_send, half_recv, back_send, back_recv,
+    send_buf, recv_buf, half_send, half_own, half_recv, back_send, back_recv,
     sound, mass, dens, vel, lab, sidx, sval, flat, mixed, large, turned_large,
     base_v, coef_v, base_d, coef_d, corr, row_of, col_of,
     send_sem, recv_sem, half_sem, half_got, back_sem, back_got, load_sem,
@@ -134,20 +134,26 @@
 
     own_low = lax.div(gx, 2)
     neighbour = (gz, gx + 2 - 4 * own_low)
+    high, plane_x, plane_y = lax.div(gz, 16), lax.rem(lax.div(gz, 4), 4), lax.rem(gz, 4)
+    ring = (2, 3, 1, 0)
+    rows_y = [lax.rem(plane_y + o, 4) for o in ring]
 
     def each_peer(visit):
-        def place(at, carry):
+        def line(step, carry):
+            t, u = lax.div(step, 4), lax.rem(step, 4)
+            far_z = lax.rem(high + 2 + lax.div(t * (t + 1), 2), 4)
+            far_x = lax.rem(plane_x + 2 + lax.div(u * (u + 1), 2), 4)
+            for y in rows_y:
+                at = far_z * 16 + far_x * 4 + y
+                for low in range(2):
+                    visit(at, low, (at, 2 * low + core))
+            return carry
+
+        lax.fori_loop(0, 15, line, 0)
+        for y in rows_y[:3]:
+            at = high * 16 + plane_x * 4 + y
             for low in range(2):
                 visit(at, low, (at, 2 * low + core))
-            return carry
-
-        def pair(step, carry):
-            place(lax.rem(gz + 32 + step, 64), 0)
-            place(lax.rem(gz + 32 - step, 64), 0)
-            return carry
-
-        place(lax.rem(gz + 32, 64), 0)
-        lax.fori_loop(1, 32, pair, 0)
         visit(gz, 1 - own_low, neighbour)
 
     barrier = pltpu.get_barrier_semaphore()
@@ -211,16 +217,17 @@
     def combine(u, v, mask):
         return jnp.where(mask, u, v) + pltpu.roll(jnp.where(mask, v, u), 64, 1)
 
-    def get_slab(which):
-        folds = ([], [])
+    core_sign = (1 - 2 * core).astype(F32)
+
+    def get_slab(which, own):
+        blocks = []
         for tile in range(2):
             near = [recv_buf[which, pl.ds(tile + 8 * at, 64, stride=16), :] for at in range(2)]
-            for blocks, sign in zip(folds, (1, -1)):
-                b0, b1 = interleave(*[a[:32] + sign * a[32:] for a in near])
-                q0, q2 = both(b0)
-                q1, q3 = both(b1)
-                blocks += [q0, q1, q2, q3]
-        return [stacked(blocks) for blocks in folds]
+            b0, b1 = interleave(*[a[:32] + (core_sign if own else -core_sign) * a[32:] for a in near])
+            q0, q2 = both(b0)
+            q1, q3 = both(b1)
+            blocks += [q0, q1, q2, q3]
+        return stacked(blocks)
 
     def put_slab(which, folds):
         for tile in range(2):
@@ -231,17 +238,19 @@
             for at in range(2):
                 first = tile + 8 * at
                 send_buf[which, pl.ds(first, 32, stride=16), :] = ends[0][at] + ends[1][at]
-                send_buf[which, pl.ds(first + 512, 32, stride=16), :] = ends[0][at] - ends[1][at]
-
-    def along_z(table, folds):
-        return [long_product((table[h, 0], table[h, 1]), folds[h]) for h in range(2)]
-
-
-    def give_half(which, value):
-        for half in range(2):
-            half_send[which, half] = combine(value[half][:128], value[half][128:], low)
+                send_buf[which, pl.ds(first + 512, 32, stride=16), :] = core_sign * (
+                    ends[0][at] - ends[1][at]
+                )
+
+    def along_z(table, value, own):
+        half = core if own else 1 - core
+        return long_product((table[half, 0], table[half, 1]), value)
+
+    def give_half(which, make):
+        value = make(False)
+        half_send[which] = combine(value[:128], value[128:], low)
         copy = pltpu.make_async_remote_copy(
-            half_send.at[which, 1 - core],
+            half_send.at[which],
             half_recv.at[which],
             half_sem.at[which],
             half_got.at[which],
@@ -249,11 +258,13 @@
             device_id_type=MESH,
         )
         copy.start()
+        value = make(True)
+        half_own[which] = combine(value[:128], value[128:], low)
         return copy
 
     def take_half(which, copy):
         copy.wait_recv()
-        mine = half_send[which, core]
+        mine = half_own[which]
         other = half_recv[which]
         top = jnp.where(low, mine, pltpu.roll(other, 64, 1))
         bottom = jnp.where(low, pltpu.roll(mine, 64, 1), other)
@@ -261,22 +272,21 @@
 
     def give_back(which, value):
         top, bottom = value[:128], value[128:]
-        back_recv[which, core] = jnp.where(low, top, pltpu.roll(bottom, 64, 1))
         back_send[which] = jnp.where(low, pltpu.roll(top, 64, 1), bottom)
         copy = pltpu.make_async_remote_copy(
             back_send.at[which],
-            back_recv.at[which, core],
+            back_recv.at[which],
             back_sem.at[which],
             back_got.at[which],
             device_id=partner,
             device_id_type=MESH,
         )
         copy.start()
-        return copy
+        return copy, stacked(both(jnp.where(low, top, pltpu.roll(bottom, 64, 1))))
 
     def take_back(which, copy):
         copy.wait_recv()
-        return [stacked(both(back_recv[which, half])) for half in range(2)]
+        return stacked(both(back_recv[which]))
 
     for load in loads[:4]:
         load.wait()
@@ -361,19 +371,21 @@
     copies = []
 
     arrived(P_S)
-    copy = give_half(P_C, along_z(r_large, get_slab(P_S)))
+    copy = give_half(P_C, lambda own: along_z(r_large, get_slab(P_S, own), own))
     copies.append(copy)
     spectrum = product(take_half(P_C, copy), r_mixed, "nt")
     spectrum = split(spectrum * corr[...])
-    back_0 = give_back(V0_I, product(spectrum, r_mixed, "nn"))
-    back_x = give_back(VX_I, product(spectrum, d_mixed, "nn"))
+    back_0, own_0 = give_back(V0_I, product(spectrum, r_mixed, "nn"))
+    back_x, own_x = give_back(VX_I, product(spectrum, d_mixed, "nn"))
     copies += [back_0, back_x]
-    field = take_back(V0_I, back_0)
-    put_slab(U0_S, along_z(r_turned, field))
+    part = along_z(r_turned, own_0, True)
+    other_0 = take_back(V0_I, back_0)
+    put_slab(U0_S, [part, along_z(r_turned, other_0, False)])
     send(U0_S)
-    put_slab(UX_S, along_z(r_turned, take_back(VX_I, back_x)))
+    part = along_z(r_turned, own_x, True)
+    put_slab(UX_S, [part, along_z(r_turned, take_back(VX_I, back_x), False)])
     send(UX_S)
-    put_slab(UZ_S, along_z(d_turned, field))
+    put_slab(UZ_S, [along_z(d_turned, own_0, True), along_z(d_turned, other_0, False)])
     send(UZ_S)
 
     where = sidx[...]
@@ -422,18 +434,19 @@
         out_v[a] = fresh.reshape(Z_LOC, X_LOC, NY)
 
     arrived(VY_S)
-    part_yz = along_z(r_large, get_slab(VY_S))
+    part_yz = [along_z(r_large, get_slab(VY_S, own), own) for own in (False, True)]
     arrived(VX_S)
-    copy_x = give_half(X_C, along_z(r_large, get_slab(VX_S)))
+    copy_x = give_half(X_C, lambda own: along_z(r_large, get_slab(VX_S, own), own))
     spectrum = product(take_half(X_C, copy_x), d_mixed, "nt")
     arrived(VZ_S)
     copy_yz = give_half(
-        YZ_C, [y - z for y, z in zip(part_yz, along_z(d_large, get_slab(VZ_S)))]
+        YZ_C, lambda own: part_yz[own] - along_z(d_large, get_slab(VZ_S, own), own)
     )
     spectrum = product(take_half(YZ_C, copy_yz), r_mixed, "nt") - spectrum
-    back_e = give_back(E_I, product(split(spectrum * corr[...]), r_mixed, "nn"))
+    back_e, own_e = give_back(E_I, product(split(spectrum * corr[...]), r_mixed, "nn"))
     copies += [copy_x, copy_yz, back_e]
-    put_slab(E_S, along_z(r_turned, take_back(E_I, back_e)))
+    part = along_z(r_turned, own_e, True)
+    put_slab(E_S, [part, along_z(r_turned, take_back(E_I, back_e), False)])
     send(E_S)
 
     arrived(E_S)
@@ -461,10 +474,11 @@
         scratch_shapes=[
             pltpu.VMEM((8, WIDE, 128), F32),
             pltpu.VMEM((8, WIDE, 128), F32),
-            pltpu.VMEM((3, 2, 128, 128), F32),
             pltpu.VMEM((3, 128, 128), F32),
             pltpu.VMEM((3, 128, 128), F32),
-            pltpu.VMEM((3, 2, 128, 128), F32),
+            pltpu.VMEM((3, 128, 128), F32),
+            pltpu.VMEM((3, 128, 128), F32),
+            pltpu.VMEM((3, 128, 128), F32),
             pltpu.SMEM((LABELS,), F32),
             pltpu.SMEM((LABELS,), F32),
             pltpu.VMEM(field, F32),

time: 62.4 us -> 58.2 us (0.933)
  Pallas kernels: 60.2 us -> 56.1 us
    pallas_call x1, Pallas kernels: 60.2 us -> 56.1 us  [shards(): pl.pallas_call(kernel, out_shape=(pltpu.VMEM(field, F32), pltpu.VMEM((3,)...]
where the time goes in v4:
time: 58.2 us; the launch traced here: 58.1 us
  Pallas kernels  56.1 us (96%)
  local copies, waits for them, and re-layouts  1.4 us (2%)
  between operations  0.64 us (1%)
    pallas_call x1, Pallas kernels, shards(): pl.pallas_call(kernel, out_shape=(pltpu.VMEM(field, F32), pltpu.VMEM((3,)...  56.1 us
    unnamed x2, local copies, waits for them, and re-layouts  1.4 us

profile of v4, /device:TPU:1, one launch (start us, length us, event | category | flops | bytes accessed | tf_op | source)
XLA Modules:
  0.0 58.1 jit_solution(8031075689708507034)
XLA Ops:
  0.6 56.1 %shard_map.104 = (f32[8,32,128]{2,1,0:T(8,128)S(1)}, f32[3,8,32,128]{3,2,1,0:T(8,128)S(1)}) custom-call(f32[8]{0:T(128)} %sound_hbm.1, f32[8]{0:T(128)} %mass_hbm.1, f32[8,32,128]{2,1,0:T(8,128)} %dens_hbm.1, f32[3,8,32,128]{3,2,1,0:T(8,128)} %vel_hbm.1, s32[8,32,128]{2,1,0:T(8,128)} %lab_hbm.1, s32[32,128]{1,0:T(8,128)} %bitcast.2, f32[32,128]{1,0:T(8,128)} %bitcast.3, ...), custom_call_target="tpu_custom_call" | custom-call | tf_op jit(solution)/shard_map/pallas_call | solution.py:466
  56.7 0.7 %copy.13 = f32[8,32,128]{2,1,0:T(8,128)} copy(f32[8,32,128]{2,1,0:T(8,128)S(1)} %get-tuple-element.2) | data formatting | bytes 262144
  57.4 0.7 %copy.14 = f32[3,8,32,128]{3,2,1,0:T(8,128)} copy(f32[3,8,32,128]{3,2,1,0:T(8,128)S(1)} %get-tuple-element.3) | data formatting | bytes 786432

commit v5 on v4

--- a/solution.py
+++ b/solution.py
@@ -139,17 +139,22 @@
     rows_y = [lax.rem(plane_y + o, 4) for o in ring]
 
     def each_peer(visit):
-        def line(step, carry):
-            t, u = lax.div(step, 4), lax.rem(step, 4)
-            far_z = lax.rem(high + 2 + lax.div(t * (t + 1), 2), 4)
-            far_x = lax.rem(plane_x + 2 + lax.div(u * (u + 1), 2), 4)
-            for y in rows_y:
-                at = far_z * 16 + far_x * 4 + y
-                for low in range(2):
-                    visit(at, low, (at, 2 * low + core))
-            return carry
-
-        lax.fori_loop(0, 15, line, 0)
+        def lines(first, last, far):
+            rows_z = [lax.rem(high + z, 4) for z in far]
+
+            def line(step, carry):
+                far_x = lax.rem(plane_x + 2 + lax.div(step * (step + 1), 2), 4)
+                for y in rows_y:
+                    for z in rows_z:
+                        at = z * 16 + far_x * 4 + y
+                        for low in range(2):
+                            visit(at, low, (at, 2 * low + core))
+                return carry
+
+            lax.fori_loop(first, last, line, 0)
+
+        lines(0, 4, (2, 3, 1))
+        lines(0, 3, (0,))
         for y in rows_y[:3]:
             at = high * 16 + plane_x * 4 + y
             for low in range(2):
@@ -458,12 +463,23 @@
         copy.wait_send()
 
 
+def write_out(new_d, new_v, out_d, out_v, out_sem):
+    copies = [
+        pltpu.make_async_copy(here, away, out_sem.at[i])
+        for i, (here, away) in enumerate(((new_v, out_v), (new_d, out_d)))
+    ]
+    for copy in copies:
+        copy.start()
+    for copy in copies:
+        copy.wait()
+
+
 def shards(density, velocity, labels, sound_table, mass_table, source_index, source_values):
     small, large = tables()
     vmem = pl.BlockSpec(memory_space=pltpu.VMEM)
     hbm = pl.BlockSpec(memory_space=pl.ANY)
     field = (Z_LOC, X_LOC, NY)
-    return pl.pallas_call(
+    results = pl.pallas_call(
         kernel,
         out_shape=(
             pltpu.VMEM(field, F32),
@@ -518,6 +534,17 @@
         jnp.asarray(large),
     )
 
+    return pl.pallas_call(
+        write_out,
+        out_shape=(
+            jax.ShapeDtypeStruct(field, F32),
+            jax.ShapeDtypeStruct((3,) + field, F32),
+        ),
+        in_specs=[vmem, vmem],
+        out_specs=(hbm, hbm),
+        scratch_shapes=[pltpu.SemaphoreType.DMA((2,))],
+    )(*[pltpu.with_memory_space_constraint(result, pltpu.VMEM) for result in results])
+
 
 def solution(mesh):
     in_specs = (

time: 58.2 us -> 57.4 us (0.986)
  local copies, waits for them, and re-layouts: 1.4 us -> 0 us
  Pallas kernels: 56.1 us -> 56.7 us
    unnamed x2 -> x0, local copies, waits for them, and re-layouts: 1.4 us -> none
    pallas_call x0 -> x1, Pallas kernels: none -> 0.8 us  [shards(): pl.pallas_call(write_out, out_shape=(jax.ShapeDtypeStruct(field, F32), ja...]
where the time goes in v5:
time: 57.4 us; the launch traced here: 57.3 us
  Pallas kernels  56.7 us (99%)
  between operations  0.64 us (1%)
    pallas_call x1, Pallas kernels, shards(): pl.pallas_call(kernel, out_shape=(pltpu.VMEM(field, F32), pltpu.VMEM((3,)...  55.9 us

profile of v5, /device:TPU:1, one launch (start us, length us, event | category | flops | bytes accessed | tf_op | source)
XLA Modules:
  0.0 57.3 jit_solution(14514449560309833610)
XLA Ops:
  0.6 55.9 %shard_map.104 = (f32[8,32,128]{2,1,0:T(8,128)S(1)}, f32[3,8,32,128]{3,2,1,0:T(8,128)S(1)}) custom-call(f32[8]{0:T(128)} %sound_hbm.1, f32[8]{0:T(128)} %mass_hbm.1, f32[8,32,128]{2,1,0:T(8,128)} %dens_hbm.1, f32[3,8,32,128]{3,2,1,0:T(8,128)} %vel_hbm.1, s32[8,32,128]{2,1,0:T(8,128)} %lab_hbm.1, s32[32,128]{1,0:T(8,128)} %bitcast.2, f32[32,128]{1,0:T(8,128)} %bitcast.3, ...), custom_call_target="tpu_custom_call" | custom-call | tf_op jit(solution)/shard_map/pallas_call | solution.py:482
  56.5 0.8 %shard_map.105 = (f32[8,32,128]{2,1,0:T(8,128)}, f32[3,8,32,128]{3,2,1,0:T(8,128)}) custom-call(f32[8,32,128]{2,1,0:T(8,128)S(1)} %get-tuple-element.4.new_d, f32[3,8,32,128]{3,2,1,0:T(8,128)S(1)} %get-tuple-element.5.new_v), custom_call_target="tpu_custom_call" | custom-call | tf_op jit(solution)/shard_map/pallas_call | solution.py:537

commit v6 on v5

--- a/solution.py
+++ b/solution.py
@@ -466,7 +466,10 @@
 def write_out(new_d, new_v, out_d, out_v, out_sem):
     copies = [
         pltpu.make_async_copy(here, away, out_sem.at[i])
-        for i, (here, away) in enumerate(((new_v, out_v), (new_d, out_d)))
+        for i, (here, away) in enumerate(
+            [(new_v.at[a, pl.ds(h, 4)], out_v.at[a, pl.ds(h, 4)]) for a in range(3) for h in (0, 4)]
+            + [(new_d.at[pl.ds(h, 4)], out_d.at[pl.ds(h, 4)]) for h in (0, 4)]
+        )
     ]
     for copy in copies:
         copy.start()
@@ -542,7 +545,7 @@
         ),
         in_specs=[vmem, vmem],
         out_specs=(hbm, hbm),
-        scratch_shapes=[pltpu.SemaphoreType.DMA((2,))],
+        scratch_shapes=[pltpu.SemaphoreType.DMA((8,))],
     )(*[pltpu.with_memory_space_constraint(result, pltpu.VMEM) for result in results])
 
 

time: 57.4 us -> 57.5 us (level)
  no operation moved by 1% of the time
where the time goes in v6:
time: 57.5 us; the launch traced here: 57.4 us
  Pallas kernels  56.7 us (99%)
  between operations  0.64 us (1%)
    pallas_call x1, Pallas kernels, shards(): pl.pallas_call(kernel, out_shape=(pltpu.VMEM(field, F32), pltpu.VMEM((3,)...  55.9 us

profile of v6, /device:TPU:1, one launch (start us, length us, event | category | flops | bytes accessed | tf_op | source)
XLA Modules:
  0.0 57.4 jit_solution(5329275713113271307)
XLA Ops:
  0.6 55.9 %shard_map.104 = (f32[8,32,128]{2,1,0:T(8,128)S(1)}, f32[3,8,32,128]{3,2,1,0:T(8,128)S(1)}) custom-call(f32[8]{0:T(128)} %sound_hbm.1, f32[8]{0:T(128)} %mass_hbm.1, f32[8,32,128]{2,1,0:T(8,128)} %dens_hbm.1, f32[3,8,32,128]{3,2,1,0:T(8,128)} %vel_hbm.1, s32[8,32,128]{2,1,0:T(8,128)} %lab_hbm.1, s32[32,128]{1,0:T(8,128)} %bitcast.2, f32[32,128]{1,0:T(8,128)} %bitcast.3, ...), custom_call_target="tpu_custom_call" | custom-call | tf_op jit(solution)/shard_map/pallas_call | solution.py:485
  56.5 0.9 %shard_map.105 = (f32[8,32,128]{2,1,0:T(8,128)}, f32[3,8,32,128]{3,2,1,0:T(8,128)}) custom-call(f32[8,32,128]{2,1,0:T(8,128)S(1)} %get-tuple-element.4.new_d, f32[3,8,32,128]{3,2,1,0:T(8,128)S(1)} %get-tuple-element.5.new_v), custom_call_target="tpu_custom_call" | custom-call | tf_op jit(solution)/shard_map/pallas_call | solution.py:540
